TPU v7x, 32 devices: a whole 2x2x4 slice. The times are simulated.
32 devices in a mesh: dp: 4 (over y, x), tensor: 8 (over z, core).
Axes of the slice: x: 2, y: 2, z: 4, core: 2. Of those that a mesh axis runs over, the one named last changes fastest.
Arguments:
- attention_output: bfloat16 [512, 8192], P('dp', 'tensor'), may hold values from -6 to 6
- residual: bfloat16 [512, 8192], P('dp', 'tensor'), may hold values from -6 to 6
- output_weight: bfloat16 [8192, 8192], P('tensor'), may hold values from -0.09375 to 0.09375
- down_factors: bfloat16 [256, 8192, 16], P('dp', 'tensor'), may hold values from -0.0625 to 0.0625
- up_factors: bfloat16 [256, 16, 8192], P('dp', None, 'tensor'), may hold values from -1.5 to 1.5
- adapter_index: int32 [512], P('dp'), may hold values from 0 to 255, as said below
Outputs:
- layer_out: bfloat16 [512, 8192], P('dp', 'tensor')
Inputs may be any that keep to these rules, and one draw needn't show every extreme that they name: adapter_index // 64 is the request group that owns the adapter. Of one group's 128 rows at most 64 use adapters owned by one group, and in every draw some group owns the adapters of exactly 64 rows of every group.
All inputs are finite; a program needn't handle non-finite values.
Results may differ from a plain program's by a relative error of at most 0.0041.
Values may be sent and summed in bfloat16 or wider, within the bound.
A program may use at most 64 MiB of HBM per device.

v0:
```python
import jax
import jax.numpy as jnp
from jax import lax
from jax.sharding import PartitionSpec as P


def body(attention_output, residual, output_weight, down_factors, up_factors, adapter_index):
    row_count = attention_output.shape[0]
    portion_width = attention_output.shape[1]
    column_count = output_weight.shape[1] // lax.axis_size("tensor")
    owned_total = down_factors.shape[0]
    rank_extent = down_factors.shape[2]
    groups = lax.axis_size("dp")
    capacity = 2 * row_count // groups
    slot_count = groups * capacity
    base_out = lax.psum_scatter(
        lax.dot_general(
            output_weight,
            attention_output,
            (((0,), (1,)), ((), ())),
            preferred_element_type=jnp.float32,
        ),
        "tensor",
        scatter_dimension=0,
        tiled=True,
    ).T
    owner_group = adapter_index // owned_total
    local_index = adapter_index % owned_total
    owner_hot = (owner_group[:, None] == jnp.arange(groups)[None, :]).astype(jnp.int32)
    slot_ids = jnp.arange(slot_count)
    rank_rows = jnp.cumsum(owner_hot, axis=0) - owner_hot
    row_slot = jnp.sum(rank_rows * owner_hot, axis=1) + owner_group * capacity
    placing = slot_ids[:, None] == row_slot[None, :]
    request = jnp.sum(jnp.where(placing, (local_index + 1)[None, :], 0), axis=1)
    request = request.astype(jnp.bfloat16).reshape(groups, capacity)
    numbers = (jnp.arange(owned_total) + 1).astype(jnp.bfloat16)
    outgoing = jnp.dot(
        placing.astype(jnp.bfloat16), attention_output, preferred_element_type=jnp.float32
    ).astype(jnp.bfloat16)
    outgoing = outgoing.reshape(groups, capacity, portion_width)
    x_slots = lax.all_to_all(outgoing, "dp", split_axis=0, concat_axis=0, tiled=True)
    wanted = lax.all_to_all(request, "dp", split_axis=0, concat_axis=0, tiled=True)
    per_source = x_slots.shape[1]
    slot_total = groups * per_source
    flat_rows = x_slots.reshape(slot_total, portion_width)
    chosen = (wanted.reshape(slot_total, 1) == numbers[None, :]).astype(jnp.bfloat16)
    all_terms = jnp.einsum(
        "nk,akj->naj", flat_rows, down_factors, preferred_element_type=jnp.float32
    )
    shrink = jnp.sum(all_terms * chosen.astype(jnp.float32)[:, :, None], axis=1)
    shrink = lax.psum(shrink, "tensor").astype(jnp.bfloat16)
    spread = (chosen[:, :, None] * shrink[:, None, :]).reshape(
        slot_total, owned_total * rank_extent
    )
    expand = jnp.dot(
        spread,
        up_factors.reshape(owned_total * rank_extent, column_count),
        preferred_element_type=jnp.float32,
    )
    expand = expand.astype(jnp.bfloat16).reshape(groups, per_source, column_count)
    returned = lax.all_to_all(expand, "dp", split_axis=0, concat_axis=0, tiled=True)
    branch_out = jnp.take(returned.reshape(slot_count, column_count), row_slot, axis=0).astype(
        jnp.float32
    )
    total = residual.astype(jnp.float32) + base_out + branch_out
    return total.astype(jnp.bfloat16)


def solution(mesh):
    return jax.shard_map(
        body,
        mesh=mesh,
        in_specs=(
            P("dp", "tensor"),
            P("dp", "tensor"),
            P("tensor", None),
            P("dp", "tensor", None),
            P("dp", None, "tensor"),
            P("dp"),
        ),
        out_specs=P("dp", "tensor"),
        check_vma=False,
    )
```

profile of v0, /device:TPU:0, one launch (start us, length us, event | category | flops | bytes accessed | tf_op | source)
XLA Modules:
  0.0 96.3 jit_solution(11963666928958346636)
XLA Ops:
  6.5 0.0 copy-start
  6.5 0.0 reduce-scatter.2.cloned.1.call-start
  6.5 12.4 %fusion.25 = f32[8192,128]{1,0:T(8,128)} fusion(bf16[1024,8192]{1,0:T(8,128)(2,1)} %param.8, bf16[128,1024]{1,0:T(8,128)(2,1)} %param.6), kind=kOutput, calls=%fused_computation.35 | convolution fusion | flops 2147483648 | bytes 21233664 | tf_op jit(solution)/shard_map/dot_general | solution.py:17
  19.0 0.0 copy-start.3
  19.0 0.0 copy-start.1
  19.0 0.0 reduce-scatter.2.cloned.1.call-update
  19.0 0.6 copy-done.3
  19.6 0.1 fusion.22
  19.7 0.2 reduce_window_sum.11
  19.9 0.2 select_reduce_fusion.1
  20.1 0.1 select_reduce_fusion
  20.2 0.7 convert_element_type.72
  20.9 5.2 %all-to-all-start = ((bf16[4,1,64]{2,1,0:T(2,128)(2,1)}), bf16[4,1,64]{2,1,0:T(2,128)(2,1)S(1)}, u32[]{:S(2)}, u32[]{:S(2)}) async-start(bf16[4,1,64]{2,1,0:T(2,128)(2,1)} %convert_element_type.72), calls=%async_computation.1 | async-start | bytes 4096 | tf_op jit(solution)/shard_map/all_to_all | solution.py:42
  26.1 0.0 copy-done.1
  26.1 1.1 %convolution_convert_fusion = bf16[256,1024]{1,0:T(8,128)(2,1)} fusion(bf16[128,1024]{1,0:T(8,128)(2,1)S(1)} %copy-done.1, s32[128]{0:T(128)S(1)} %get-tuple-element.6), kind=kOutput, calls=%fused_computation.8 | convolution fusion | flops 67403776 | bytes 786944 | tf_op jit(solution)/shard_map/dot_general | solution.py:37
  27.2 3.5 %all-to-all-done = bf16[4,1,64]{2,1,0:T(2,128)(2,1)S(1)} async-done(((bf16[4,1,64]{2,1,0:T(2,128)(2,1)}), bf16[4,1,64]{2,1,0:T(2,128)(2,1)S(1)}, u32[]{:S(2)}, u32[]{:S(2)}) %all-to-all-start) | async-done | bytes 544 | tf_op jit(solution)/shard_map/all_to_all | solution.py:42
  30.7 3.5 %all-to-all-start.1 = ((bf16[4,64,1024]{2,1,0:T(8,128)(2,1)}), bf16[4,64,1024]{2,1,0:T(8,128)(2,1)S(1)}, u32[]{:S(2)}, u32[]{:S(2)}) async-start(bf16[4,64,1024]{2,1,0:T(8,128)(2,1)} %bitcast.1), calls=%async_computation.2 | async-start | bytes 1048576 | tf_op jit(solution)/shard_map/all_to_all | solution.py:41
  34.2 0.1 eq.56
  34.3 0.1 compare_convert_fusion
  34.3 6.7 %all-to-all-done.1 = bf16[4,64,1024]{2,1,0:T(8,128)(2,1)S(1)} async-done(((bf16[4,64,1024]{2,1,0:T(8,128)(2,1)}), bf16[4,64,1024]{2,1,0:T(8,128)(2,1)S(1)}, u32[]{:S(2)}, u32[]{:S(2)}) %all-to-all-start.1) | async-done | bytes 524320 | tf_op jit(solution)/shard_map/all_to_all | solution.py:41
  41.0 4.1 %fusion.13 = f32[256,16]{0,1:T(8,128)S(1)} fusion(bf16[256,1024,1]{1,0,2:T(8,128)(2,1)S(1)} %bitcast.21, bf16[64,1024,16]{1,2,0:T(8,128)(2,1)} %param.9, f32[256,64]{0,1:T(8,128)S(1)} %get-tuple-element.8), kind=kOutput, calls=%fused_computation.9 | convolution fusion | flops 537391104 | bytes 2703360 | tf_op jit(solution)/shard_map/nk,akj->naj/dot_general | solution.py:47
  45.1 28.0 %psum.7 = bf16[256,16]{0,1:T(8,128)(2,1)S(1)} all-reduce(f32[256,16]{0,1:T(8,128)S(1)} %fusion.13), channel_id=1, replica_groups=mesh['dp'=4,'tensor'=8] {'tensor'}, use_global_device_ids=true, to_apply=%region_5.6 | all-reduce | flops 4096 | bytes 24576 | tf_op jit(solution)/shard_map/psum | solution.py:51
  73.0 0.0 copy-done
  73.1 0.0 copy-start.2
  73.1 3.3 %fusion.10 = bf16[256,1024]{1,0:T(8,128)(2,1)} fusion(bf16[64,16,1024]{2,1,0:T(8,128)(2,1)S(1)} %copy-done, bf16[256,16]{0,1:T(8,128)(2,1)S(1)} %psum.7, bf16[256,64]{0,1:T(8,128)(2,1)S(1)} %get-tuple-element.7), kind=kOutput, calls=%fused_computation.7 | convolution fusion | flops 537395200 | bytes 2662400 | tf_op jit(solution)/shard_map/dot_general | solution.py:55
  76.4 3.5 %all-to-all-start.2 = ((bf16[4,64,1024]{2,1,0:T(8,128)(2,1)}), bf16[4,64,1024]{2,1,0:T(8,128)(2,1)S(1)}, u32[]{:S(2)}, u32[]{:S(2)}) async-start(bf16[4,64,1024]{2,1,0:T(8,128)(2,1)} %bitcast.5), calls=%async_computation.3 | async-start | bytes 1048576 | tf_op jit(solution)/shard_map/all_to_all | solution.py:61
  79.9 0.0 copy-done.2
  79.9 0.2 copy.23
  80.1 6.3 %all-to-all-done.2 = bf16[4,64,1024]{2,1,0:T(8,128)(2,1)S(1)} async-done(((bf16[4,64,1024]{2,1,0:T(8,128)(2,1)}), bf16[4,64,1024]{2,1,0:T(8,128)(2,1)S(1)}, u32[]{:S(2)}, u32[]{:S(2)}) %all-to-all-start.2) | async-done | bytes 524320 | tf_op jit(solution)/shard_map/all_to_all | solution.py:61
  86.4 0.9 gather_fusion
  87.3 0.2 copy.27
  87.5 0.0 reduce-scatter.2.cloned.1.call-done
  87.5 1.2 %fusion.17 = bf16[128,1024]{0,1:T(8,128)(2,1)S(1)} fusion(f32[1024,128]{1,0:T(8,128)} %reduce-scatter.2.cloned.1.call-done, bf16[128,1024]{0,1:T(8,128)(2,1)S(1)} %copy.23, bf16[128,1024]{0,1:T(8,128)(2,1)S(1)} %copy.27, pred[128]{0:T(512)(128)(4,1)S(1)} %get-tuple-element.5), kind=kLoop, calls=%fused_computation.12 | loop fusion | flops 786432 | bytes 1310848 | tf_op jit(solution)/shard_map/convert_element_type | solution.py:66
  88.6 0.9 copy.28
  (7 shorter events, 0.1 us)
Async XLA Ops:
  6.5 66.5 %copy-start = (bf16[64,16,1024]{2,1,0:T(8,128)(2,1)S(1)}, bf16[64,16,1024]{2,1,0:T(8,128)(2,1)}, u32[]{:S(2)}) copy-start(bf16[64,16,1024]{2,1,0:T(8,128)(2,1)} %param.10) | copy-start | bytes 6291460
  6.5 80.9 %reduce-scatter.2.cloned.1.call-start = ((), (), s32[]{:S(2)}) async-start(), calls=%async_computation.4 | async-start | bytes 4718592 | tf_op jit(solution)/shard_map/reduce_scatter | solution.py:16
  19.0 0.7 copy-start.3
  19.0 7.1 %copy-start.1 = (bf16[128,1024]{1,0:T(8,128)(2,1)S(1)}, bf16[128,1024]{1,0:T(8,128)(2,1)}, u32[]{:S(2)}) copy-start(bf16[128,1024]{1,0:T(8,128)(2,1)} %param.6) | copy-start | bytes 786436
  20.9 9.8 %all-to-all-start = ((bf16[4,1,64]{2,1,0:T(2,128)(2,1)}), bf16[4,1,64]{2,1,0:T(2,128)(2,1)S(1)}, u32[]{:S(2)}, u32[]{:S(2)}) async-start(bf16[4,1,64]{2,1,0:T(2,128)(2,1)} %convert_element_type.72), calls=%async_computation.1 | async-start | bytes 4096 | tf_op jit(solution)/shard_map/all_to_all | solution.py:42
  30.7 10.4 %all-to-all-start.1 = ((bf16[4,64,1024]{2,1,0:T(8,128)(2,1)}), bf16[4,64,1024]{2,1,0:T(8,128)(2,1)S(1)}, u32[]{:S(2)}, u32[]{:S(2)}) async-start(bf16[4,64,1024]{2,1,0:T(8,128)(2,1)} %bitcast.1), calls=%async_computation.2 | async-start | bytes 1048576 | tf_op jit(solution)/shard_map/all_to_all | solution.py:41
  73.1 6.8 %copy-start.2 = (bf16[128,1024]{1,0:T(8,128)(2,1)S(1)}, bf16[128,1024]{1,0:T(8,128)(2,1)}, u32[]{:S(2)}) copy-start(bf16[128,1024]{1,0:T(8,128)(2,1)} %param.7) | copy-start | bytes 786436
  76.4 10.0 %all-to-all-start.2 = ((bf16[4,64,1024]{2,1,0:T(8,128)(2,1)}), bf16[4,64,1024]{2,1,0:T(8,128)(2,1)S(1)}, u32[]{:S(2)}, u32[]{:S(2)}) async-start(bf16[4,64,1024]{2,1,0:T(8,128)(2,1)} %bitcast.5), calls=%async_computation.3 | async-start | bytes 1048576 | tf_op jit(solution)/shard_map/all_to_all | solution.py:61
Sparse Core Ops, SparseCore 0:
  19.1 53.1 reduce-scatter.1
where the time goes:
time: 96.7 us; the launch traced here: 96.3 us
  blocking collectives  28 us (29%)
  matrix products  20.9 us (22%)
  waiting for transfers between devices  16.5 us (17%)
  between operations  13.5 us (14%)
  starting transfers between devices  12.1 us (13%)
  local copies, waits for them, and re-layouts  3.45 us (4%)
  other arithmetic  1.86 us (2%)
    psum x1, blocking collectives, body(): shrink = lax.psum(shrink, 'tensor').astype(jnp.bfloat16)  28 us
    dot_general x1, matrix products, body(): lax.dot_general(output_weight, attention_output, (((0,), (1,)), ((), ()))...  12.4 us
    all_to_all x1, waiting for transfers between devices, body(): lax.all_to_all(outgoing, 'dp', split_axis=0, concat_axis=0, tiled=True)  6.67 us
    all_to_all x1, waiting for transfers between devices, body(): lax.all_to_all(expand, 'dp', split_axis=0, concat_axis=0, tiled=True)  6.33 us
    all_to_all x1, starting transfers between devices, body(): lax.all_to_all(request, 'dp', split_axis=0, concat_axis=0, tiled=True)  5.19 us
    dot_general x1, matrix products, body(): jnp.einsum('nk,akj->naj', flat_rows, down_factors, preferred_element_type...  4.07 us
    all_to_all x1, waiting for transfers between devices, body(): lax.all_to_all(request, 'dp', split_axis=0, concat_axis=0, tiled=True)  3.49 us
    all_to_all x1, starting transfers between devices, body(): lax.all_to_all(outgoing, 'dp', split_axis=0, concat_axis=0, tiled=True)  3.47 us
  transfers between devices with their start and end apart: 4, of which 3 were waited for; matrix products, arithmetic and copies ran while one was open for 12% of the time, Pallas kernels for 0%

commit v1 on v0

v1 whole, which is shorter than its diff:
```python
import functools

import jax
import jax.numpy as jnp
from jax import lax
from jax.experimental import pallas as pl
from jax.experimental.pallas import tpu as pltpu
from jax.sharding import PartitionSpec as P

MESH = pl.DeviceIdType.MESH
F32 = jnp.float32
BF16 = jnp.bfloat16
LANES = 128
PIECES = 2


def kernel(
    groups, members, rank, owned,
    x_ref, res_ref, idx_ref, w_ref, down_ref, up_ref, out_ref,
    wbuf, dbuf, ubuf, own, psend, precv, rrecv, lrecv, rsend, lsend,
    xsend, xrecv, terms, packed, arp, arz, esend, eback,
    w_sem, d_sem, ps_sem, pr_sem, rs_sem, rr_sem, ls_sem, lr_sem,
    xs_sem, xr_sem, as_sem, ar_sem, zs_sem, zr_sem, es_sem, er_sem,
):
    chips = members // 2
    g = lax.axis_index("dp")
    t = lax.axis_index("tensor")
    z = t // 2
    c = lax.rem(t, 2)
    partner = z * 2 + (1 - c)
    rows, depth = x_ref.shape
    width = out_ref.shape[1]
    cap = xrecv.shape[1]
    slots = groups * cap
    low = z < chips // 2

    def block_chip(i):
        return jnp.where(low, chips - 1 - i, i)

    def weight_copy(i, which):
        column = block_chip(i) * 2 + jnp.where(which == 0, 1 - c, c)
        start = pl.multiple_of(column * width, LANES)
        return pltpu.make_async_copy(
            w_ref.at[:, pl.ds(start, width)], wbuf.at[2 * i + which], w_sem.at[2 * i + which]
        )

    down_copy = pltpu.make_async_copy(down_ref, dbuf, d_sem.at[0])
    up_copy = pltpu.make_async_copy(up_ref, ubuf, d_sem.at[1])
    for i in range(chips):
        for which in range(2):
            weight_copy(i, which).start()
        if i == 0:
            down_copy.start()
    up_copy.start()

    barrier = pltpu.get_barrier_semaphore()
    pl.semaphore_signal(barrier, inc=1, device_id=(g, partner), device_id_type=MESH)
    for k in range(1, chips):
        peer = lax.rem(z + k, chips) * 2 + c
        pl.semaphore_signal(barrier, inc=1, device_id=(g, peer), device_id_type=MESH)
    for k in range(1, groups):
        pl.semaphore_signal(
            barrier, inc=1, device_id=(lax.rem(g + k, groups), t), device_id_type=MESH
        )

    idx_row = idx_ref[...]
    r_i = lax.broadcasted_iota(jnp.int32, (rows, rows), 0)
    c_i = lax.broadcasted_iota(jnp.int32, (rows, rows), 1)
    idx_full = jnp.broadcast_to(idx_row, (rows, rows))
    idx_col = jnp.sum(jnp.where(r_i == c_i, idx_full, 0), axis=1, keepdims=True)
    own_row = idx_row // owned
    own_col = idx_col // owned
    same = own_col == own_row
    rank_row = jnp.sum(jnp.where(same & (r_i < c_i), 1, 0), axis=0, keepdims=True)
    rank_col = jnp.sum(jnp.where(same & (c_i < r_i), 1, 0), axis=1, keepdims=True)
    slot_row = rank_row + own_row * cap
    slot_col = rank_col + own_col * cap
    number_row = lax.rem(idx_row, owned) + 1
    placing = lax.broadcasted_iota(jnp.int32, (slots, rows), 0) == slot_row
    request = jnp.sum(jnp.where(placing, number_row, 0), axis=1, keepdims=True)
    place = jnp.where(placing, 1.0, 0.0).astype(BF16)
    for k in range(groups):
        xsend[k, :, depth:] = jnp.broadcast_to(
            request[k * cap:(k + 1) * cap].astype(F32), (cap, LANES)
        ).astype(BF16)
    step = min(256, depth)
    for j in range(depth // step):
        moved = jnp.dot(
            place, x_ref[:, j * step:(j + 1) * step], preferred_element_type=F32
        ).astype(BF16)
        for k in range(groups):
            xsend[k, :, j * step:(j + 1) * step] = moved[k * cap:(k + 1) * cap]

    pl.semaphore_wait(barrier, chips + groups - 1)

    def row_copy(k):
        to = lax.rem(g + k, groups)
        return pltpu.make_async_remote_copy(
            src_ref=xsend.at[to], dst_ref=xrecv.at[g], send_sem=xs_sem.at[k - 1],
            recv_sem=xr_sem.at[g], device_id=(to, t), device_id_type=MESH,
        )

    def row_wait(k):
        source = lax.rem(g + k, groups)
        pltpu.make_async_remote_copy(
            src_ref=xsend.at[source], dst_ref=xrecv.at[source], send_sem=xs_sem.at[k - 1],
            recv_sem=xr_sem.at[source], device_id=(source, t), device_id_type=MESH,
        ).wait_recv()

    for k in range(1, groups):
        row_copy(k).start()
    xrecv[g] = xsend[g]

    tile = min(256, width)
    tiles = width // tile

    def pair_copy(chip):
        return pltpu.make_async_remote_copy(
            src_ref=psend.at[chip], dst_ref=precv.at[chip], send_sem=ps_sem.at[chip],
            recv_sem=pr_sem.at[chip], device_id=(g, partner), device_id_type=MESH,
        )

    def project(i):
        chip = block_chip(i)
        weight_copy(i, 0).wait()

        @pl.loop(0, tiles)
        def _(n):
            cols = pl.ds(pl.multiple_of(n * tile, LANES), tile)
            psend[chip, :, cols] = jnp.dot(
                x_ref[...], wbuf[2 * i, :, cols], preferred_element_type=F32
            ).astype(BF16)

        pair_copy(chip).start()
        weight_copy(i, 1).wait()

        @pl.loop(0, tiles)
        def _(n):
            cols = pl.ds(pl.multiple_of(n * tile, LANES), tile)
            own[chip, :, cols] = jnp.dot(
                x_ref[...], wbuf[2 * i + 1, :, cols], preferred_element_type=F32
            )

    piece = rows // PIECES
    strip = 16

    def hop(chip, q, to, send, recv, s_sem, r_sem):
        k = chip * PIECES + q
        part = pl.ds(q * piece, piece)
        return pltpu.make_async_remote_copy(
            src_ref=send.at[chip, part], dst_ref=recv.at[chip, part], send_sem=s_sem.at[k],
            recv_sem=r_sem.at[k], device_id=(g, to * 2 + c), device_id_type=MESH,
        )

    right = functools.partial(hop, send=rsend, recv=rrecv, s_sem=rs_sem, r_sem=rr_sem)
    left = functools.partial(hop, send=lsend, recv=lrecv, s_sem=ls_sem, r_sem=lr_sem)

    def pass_on(chip, q, first, to, make, send, recv):
        @pl.when(first)
        def _():
            @pl.loop(0, piece // strip)
            def _(n):
                at = pl.ds(pl.multiple_of(q * piece + n * strip, strip), strip)
                send[chip, at] = (own[chip, at] + precv[chip, at].astype(F32)).astype(BF16)

        @pl.when(jnp.logical_not(first))
        def _():
            make(chip, q, to).wait_recv()

            @pl.loop(0, piece // strip)
            def _(n):
                at = pl.ds(pl.multiple_of(q * piece + n * strip, strip), strip)
                send[chip, at] = (
                    own[chip, at] + precv[chip, at].astype(F32) + recv[chip, at].astype(F32)
                ).astype(BF16)

        make(chip, q, to).start()

    def chain(turn, q):
        @pl.when(z <= turn)
        def _():
            pass_on(chips - 1 - turn + z, q, z == 0, z + 1, right, rsend, rrecv)

        @pl.when(chips - 1 - z <= turn)
        def _():
            pass_on(turn - chips + 1 + z, q, z == chips - 1, z - 1, left, lsend, lrecv)

    project(0)
    if chips > 1:
        project(1)
    pair_copy(block_chip(0)).wait_recv()
    for q in range(PIECES):
        chain(0, q)
    for i in range(2, chips):
        project(i)
    for i in range(1, chips):
        pair_copy(block_chip(i)).wait_recv()
    if chips > 2:
        chain(1, 0)

    for k in range(1, groups):
        row_wait(k)
    down_copy.wait()
    lane_group = lax.broadcasted_iota(jnp.int32, (slots, LANES), 1) // rank
    lane_number = (lane_group + 1).astype(F32)
    per_tile = LANES // rank
    tile_count = owned * rank // LANES
    wanted = xrecv[:, :, depth:].reshape(slots, LANES).astype(F32)
    flat = xrecv[:, :, :depth].reshape(slots, depth)
    terms[...] = jnp.zeros_like(terms)
    pair = 2 if tile_count % 2 == 0 else 1

    @pl.loop(0, tile_count // pair)
    def _(m):
        at = pl.ds(pl.multiple_of(m * pair * LANES, LANES), pair * LANES)
        every = lax.dot_general(
            flat, dbuf[at, :], (((1,), (1,)), ((), ())), preferred_element_type=F32
        )
        for p in range(pair):
            first_number = ((m * pair + p) * per_tile).astype(F32)
            terms[...] += jnp.where(
                wanted == lane_number + first_number, every[:, p * LANES:(p + 1) * LANES], 0.0
            )

    def spread_lanes(v):
        shift = rank
        while shift < LANES:
            v = v + pltpu.roll(v, shift, 1)
            shift *= 2
        return v

    pack_rows = slots // per_tile
    pack_group = lax.broadcasted_iota(jnp.int32, (pack_rows, LANES), 1) // rank
    chosen_terms = spread_lanes(terms[...])
    mine = jnp.zeros((pack_rows, LANES), F32)
    for p in range(per_tile):
        mine = jnp.where(
            pack_group == p, chosen_terms[p * pack_rows:(p + 1) * pack_rows], mine
        )
    packed[...] = mine
    term_pair = pltpu.make_async_remote_copy(
        src_ref=packed, dst_ref=arp, send_sem=as_sem.at[0], recv_sem=ar_sem.at[0],
        device_id=(g, partner), device_id_type=MESH,
    )
    term_pair.start()
    if chips > 2:
        for q in range(1, PIECES):
            chain(1, q)
    term_pair.wait_recv()
    arz[z] = packed[...] + arp[...]

    def term_copy(k):
        to = lax.rem(z + k, chips)
        return pltpu.make_async_remote_copy(
            src_ref=arz.at[z], dst_ref=arz.at[z], send_sem=zs_sem.at[k - 1],
            recv_sem=zr_sem.at[z], device_id=(g, to * 2 + c), device_id_type=MESH,
        )

    def term_wait(k):
        source = lax.rem(z + k, chips)
        pltpu.make_async_remote_copy(
            src_ref=arz.at[source], dst_ref=arz.at[source], send_sem=zs_sem.at[k - 1],
            recv_sem=zr_sem.at[source], device_id=(g, source * 2 + c), device_id_type=MESH,
        ).wait_recv()

    for k in range(1, chips):
        term_copy(k).start()
    for k in range(1, chips):
        term_wait(k)
    total = arz[0]
    for k in range(1, chips):
        total = total + arz[k]
    total = total.astype(BF16).astype(F32)

    up_copy.wait()
    shrink = jnp.concatenate(
        [spread_lanes(jnp.where(pack_group == p, total, 0.0)) for p in range(per_tile)], axis=0
    )
    spread = jnp.concatenate(
        [
            jnp.where(wanted == lane_number + float(m * per_tile), shrink, 0.0).astype(BF16)
            for m in range(tile_count)
        ],
        axis=1,
    )

    @pl.loop(0, tiles)
    def _(n):
        cols = pl.ds(pl.multiple_of(n * tile, LANES), tile)
        grown = jnp.dot(spread, ubuf[:, cols], preferred_element_type=F32).astype(BF16)
        for k in range(groups):
            esend[k, :, cols] = grown[k * cap:(k + 1) * cap]

    def back_copy(k):
        to = lax.rem(g + k, groups)
        return pltpu.make_async_remote_copy(
            src_ref=esend.at[to], dst_ref=eback.at[g], send_sem=es_sem.at[k - 1],
            recv_sem=er_sem.at[g], device_id=(to, t), device_id_type=MESH,
        )

    def back_wait(k):
        source = lax.rem(g + k, groups)
        pltpu.make_async_remote_copy(
            src_ref=esend.at[source], dst_ref=eback.at[source], send_sem=es_sem.at[k - 1],
            recv_sem=er_sem.at[source], device_id=(source, t), device_id_type=MESH,
        ).wait_recv()

    for k in range(1, groups):
        back_copy(k).start()
    eback[g] = esend[g]

    for turn in range(2, chips - 1):
        for q in range(PIECES):
            chain(turn, q)

    for k in range(1, groups):
        back_wait(k)
    unplace = jnp.where(
        lax.broadcasted_iota(jnp.int32, (rows, slots), 1) == slot_col, 1.0, 0.0
    ).astype(BF16)

    @pl.loop(0, tiles)
    def _(n):
        cols = pl.ds(pl.multiple_of(n * tile, LANES), tile)
        back = eback[:, :, cols].reshape(slots, tile)
        branch = jnp.dot(unplace, back, preferred_element_type=F32)
        own[z, :, cols] = (
            own[z, :, cols] + precv[z, :, cols].astype(F32)
            + res_ref[:, cols].astype(F32) + branch
        )

    for q in range(PIECES):
        part = slice(q * piece, (q + 1) * piece)

        @pl.when(z > 0)
        def _():
            right(z, q, z).wait_recv()

            @pl.loop(0, piece // strip)
            def _(n):
                at = pl.ds(pl.multiple_of(q * piece + n * strip, strip), strip)
                own[z, at] = own[z, at] + rrecv[z, at].astype(F32)

        @pl.when(z < chips - 1)
        def _():
            left(z, q, z).wait_recv()

            @pl.loop(0, piece // strip)
            def _(n):
                at = pl.ds(pl.multiple_of(q * piece + n * strip, strip), strip)
                own[z, at] = own[z, at] + lrecv[z, at].astype(F32)

        @pl.loop(0, piece // strip)
        def _(n):
            at = pl.ds(pl.multiple_of(q * piece + n * strip, strip), strip)
            out_ref[at] = own[z, at].astype(BF16)

    for i in range(chips):
        pair_copy(i).wait_send()
    for k in range(1, groups):
        row_copy(k).wait_send()
        back_copy(k).wait_send()
    term_pair.wait_send()
    for k in range(1, chips):
        term_copy(k).wait_send()
    for chip in range(chips):
        for q in range(PIECES):
            @pl.when(z < chip)
            def _():
                right(chip, q, z + 1).wait_send()

            @pl.when(z > chip)
            def _():
                left(chip, q, z - 1).wait_send()


def body(attention_output, residual, output_weight, down_factors, up_factors, adapter_index):
    groups = lax.axis_size("dp")
    members = lax.axis_size("tensor")
    rows, depth = attention_output.shape
    owned, _, rank = down_factors.shape
    width = output_weight.shape[1] // members
    cap = 2 * rows // groups
    chips = members // 2
    slots = groups * cap
    down = jnp.swapaxes(down_factors, 1, 2).reshape(owned * rank, depth)
    up = up_factors.reshape(owned * rank, width)
    vmem = pl.BlockSpec(memory_space=pltpu.VMEM)
    hbm = pl.BlockSpec(memory_space=pl.ANY)
    dma = pltpu.SemaphoreType.DMA
    hops = chips * PIECES
    return pl.pallas_call(
        functools.partial(kernel, groups, members, rank, owned),
        out_shape=jax.ShapeDtypeStruct((rows, width), BF16),
        in_specs=[vmem, vmem, vmem, hbm, hbm, hbm],
        out_specs=vmem,
        scratch_shapes=[
            pltpu.VMEM((members, depth, width), BF16),
            pltpu.VMEM((owned * rank, depth), BF16),
            pltpu.VMEM((owned * rank, width), BF16),
            pltpu.VMEM((chips, rows, width), F32),
            pltpu.VMEM((chips, rows, width), BF16),
            pltpu.VMEM((chips, rows, width), BF16),
            pltpu.VMEM((chips, rows, width), BF16),
            pltpu.VMEM((chips, rows, width), BF16),
            pltpu.VMEM((chips, rows, width), BF16),
            pltpu.VMEM((chips, rows, width), BF16),
            pltpu.VMEM((groups, cap, depth + LANES), BF16),
            pltpu.VMEM((groups, cap, depth + LANES), BF16),
            pltpu.VMEM((slots, LANES), F32),
            pltpu.VMEM((slots * rank // LANES, LANES), F32),
            pltpu.VMEM((slots * rank // LANES, LANES), F32),
            pltpu.VMEM((chips, slots * rank // LANES, LANES), F32),
            pltpu.VMEM((groups, cap, width), BF16),
            pltpu.VMEM((groups, cap, width), BF16),
            dma((members,)), dma((2,)),
            dma((chips,)), dma((chips,)),
            dma((hops,)), dma((hops,)), dma((hops,)), dma((hops,)),
            dma((groups,)), dma((groups,)),
            dma((1,)), dma((1,)),
            dma((chips,)), dma((chips,)),
            dma((groups,)), dma((groups,)),
        ],
        compiler_params=pltpu.CompilerParams(
            collective_id=0, has_side_effects=True, vmem_limit_bytes=60 * 1024 * 1024
        ),
    )(attention_output, residual, adapter_index.reshape(1, rows), output_weight, down, up)


def solution(mesh):
    return jax.shard_map(
        body,
        mesh=mesh,
        in_specs=(
            P("dp", "tensor"),
            P("dp", "tensor"),
            P("tensor", None),
            P("dp", "tensor", None),
            P("dp", None, "tensor"),
            P("dp"),
        ),
        out_specs=P("dp", "tensor"),
        check_vma=False,
    )
```

time: 96.7 us -> 36.9 us (0.38)
  Pallas kernels: 0 us -> 35.1 us
  blocking collectives: 28 us -> 0 us
  matrix products: 20.9 us -> 0 us
  waiting for transfers between devices: 16.5 us -> 0 us
  between operations: 13.5 us -> 0.01 us
  starting transfers between devices: 12.1 us -> 0 us
  other arithmetic: 1.86 us -> 0 us
  local copies, waits for them, and re-layouts: 3.45 us -> 1.67 us
    pallas_call x0 -> x1, Pallas kernels: none -> 35.1 us  [body(): pl.pallas_call(functools.partial(kernel, groups, members, rank, owned), o...]
    psum x1 -> x0, blocking collectives: 28 us -> none  [body(): shrink = lax.psum(shrink, 'tensor').astype(jnp.bfloat16)]
    dot_general x4 -> x0, matrix products: 20.9 us -> none  [the longest x1 12.4 us: body(): lax.dot_general(output_weight, attention_output, (((0,), (1,)), ((), ()))...]
    all_to_all x3 -> x0, waiting for transfers between devices: 16.5 us -> none  [the longest x1 6.67 us: body(): lax.all_to_all(outgoing, 'dp', split_axis=0, concat_axis=0, tiled=True)]
    all_to_all x3 -> x0, starting transfers between devices: 12.1 us -> none  [the longest x1 5.19 us: body(): lax.all_to_all(request, 'dp', split_axis=0, concat_axis=0, tiled=True)]
    convert_element_type x2 -> x0, local copies, waits for them, and re-layouts: 1.52 us -> none  [the longest x1 0.85 us: body(): return total.astype(jnp.bfloat16)]
    convert_element_type x5 -> x0, other arithmetic: 1.34 us -> none  [the longest x1 1.17 us: body(): return total.astype(jnp.bfloat16)]
    gather x2 -> x0, local copies, waits for them, and re-layouts: 1.03 us -> none  [body(): jnp.take(returned.reshape(slot_count, column_count), row_slot, axis=0)]
  transfers between devices with their start and end apart: 4 -> 0, of which waited for: 3 -> 0; matrix products, arithmetic and copies ran while one was open for 12% -> 0% of each run, Pallas kernels for 0% -> 0%
where the time goes in v1:
time: 36.9 us; the launch traced here: 36.8 us
  Pallas kernels  35.1 us (95%)
  local copies, waits for them, and re-layouts  1.67 us (5%)
    pallas_call x1, Pallas kernels, body(): pl.pallas_call(functools.partial(kernel, groups, members, rank, owned), o...  35.1 us
    unnamed x1, local copies, waits for them, and re-layouts  1.67 us

profile of v1, /device:TPU:0, one launch (start us, length us, event | category | flops | bytes accessed | tf_op | source)
XLA Modules:
  0.0 36.8 jit_solution(8624355481557222761)
XLA Ops:
  0.0 35.1 %shard_map.64 = bf16[128,1024]{1,0:T(8,128)(2,1)} custom-call(bf16[128,1024]{1,0:T(8,128)(2,1)} %x_ref.1, bf16[128,1024]{1,0:T(8,128)(2,1)} %res_ref.1, s32[1,128]{1,0:T(1,128)} %bitcast.7, bf16[1024,8192]{1,0:T(8,128)(2,1)} %w_ref.1, bf16[1024,1024]{1,0:T(8,128)(2,1)} %bitcast.5, bf16[1024,1024]{1,0:T(8,128)(2,1)} %bitcast.6), custom_call_target="tpu_custom_call" | custom-call | tf_op jit(solution)/shard_map/pallas_call | solution.py:392
  35.1 1.7 %copy.8 = bf16[128,1024]{1,0:T(8,128)(2,1)} copy(bf16[128,1024]{1,0:T(8,128)(2,1)} %shard_map.64) | data formatting | bytes 524288

commit v2 on v0

v2 whole, which is shorter than its diff:
```python
import functools

import jax
import jax.numpy as jnp
from jax import lax
from jax.experimental import pallas as pl
from jax.experimental.pallas import tpu as pltpu
from jax.sharding import PartitionSpec as P

MESH = pl.DeviceIdType.MESH
F32 = jnp.float32
BF16 = jnp.bfloat16
LANES = 128
PIECES = 2
AHEAD = 3


def kernel(
    groups, members, rank, owned, halves,
    x_ref, res_ref, idx_ref, w_ref, down_ref, up_ref, out_ref,
    wbuf, dbuf, ubuf, rbuf, own, psend, precv, rrecv, lrecv, rsend, lsend,
    xsend, xrecv, terms, packed, arp, arz, esend, eback,
    w_sem, d_sem, ps_sem, pr_sem, rs_sem, rr_sem, ls_sem, lr_sem,
    xs_sem, xr_sem, as_sem, ar_sem, zs_sem, zr_sem, es_sem, er_sem,
):
    chips = members // 2
    g = lax.axis_index("dp")
    t = lax.axis_index("tensor")
    z = t // 2
    c = lax.rem(t, 2)
    partner = z * 2 + (1 - c)
    rows, depth = x_ref.shape
    width = out_ref.shape[1]
    part = xrecv.shape[2]
    cap = part * halves
    slots = groups * part
    low = z < chips // 2
    piece = width // PIECES

    def block_chip(i):
        return jnp.where(low, chips - 1 - i, i)

    def weight_copy(n):
        column = block_chip(n // 2) * 2 + (1 - c if n % 2 == 0 else c)
        start = pl.multiple_of(column * width, LANES)
        return pltpu.make_async_copy(
            w_ref.at[:, pl.ds(start, width)], wbuf.at[n], w_sem.at[n]
        )

    down_copy = pltpu.make_async_copy(down_ref, dbuf, d_sem.at[0])
    up_copy = pltpu.make_async_copy(up_ref, ubuf, d_sem.at[1])
    res_copy = pltpu.make_async_copy(res_ref, rbuf, d_sem.at[2])
    for n in range(min(AHEAD, members)):
        weight_copy(n).start()

    barrier = pltpu.get_barrier_semaphore()
    pl.semaphore_signal(barrier, inc=1, device_id=(g, partner), device_id_type=MESH)
    for k in range(1, chips):
        peer = lax.rem(z + k, chips) * 2 + c
        pl.semaphore_signal(barrier, inc=1, device_id=(g, peer), device_id_type=MESH)
    for k in range(1, groups):
        pl.semaphore_signal(
            barrier, inc=1, device_id=(lax.rem(g + k, groups), t), device_id_type=MESH
        )

    idx_row = idx_ref[...]
    r_i = lax.broadcasted_iota(jnp.int32, (rows, rows), 0)
    c_i = lax.broadcasted_iota(jnp.int32, (rows, rows), 1)
    idx_full = jnp.broadcast_to(idx_row, (rows, rows))
    idx_col = jnp.sum(jnp.where(r_i == c_i, idx_full, 0), axis=1, keepdims=True)
    own_row = idx_row // owned
    own_col = idx_col // owned
    same = own_col == own_row
    rank_row = jnp.sum(jnp.where(same & (r_i < c_i), 1, 0), axis=0, keepdims=True)
    rank_col = jnp.sum(jnp.where(same & (c_i < r_i), 1, 0), axis=1, keepdims=True)

    def slot_of(place_rank, owner, h):
        inside = place_rank - h * part
        keep = (inside >= 0) & (inside < part)
        return jnp.where(keep, owner * part + inside, -1)

    number_row = lax.rem(idx_row, owned) + 1
    step = min(256, depth)

    def row_copy(h, k):
        to = lax.rem(g + k, groups)
        return pltpu.make_async_remote_copy(
            src_ref=xsend.at[h, to], dst_ref=xrecv.at[h, g],
            send_sem=xs_sem.at[h * groups + k], recv_sem=xr_sem.at[h * groups + g],
            device_id=(to, t), device_id_type=MESH,
        )

    def row_wait(h, k):
        source = lax.rem(g + k, groups)
        pltpu.make_async_remote_copy(
            src_ref=xsend.at[h, source], dst_ref=xrecv.at[h, source],
            send_sem=xs_sem.at[h * groups + k], recv_sem=xr_sem.at[h * groups + source],
            device_id=(source, t), device_id_type=MESH,
        ).wait_recv()

    for h in range(halves):
        slot_row = slot_of(rank_row, own_row, h)
        placing = lax.broadcasted_iota(jnp.int32, (slots, rows), 0) == slot_row
        request = jnp.sum(jnp.where(placing, number_row, 0), axis=1, keepdims=True)
        place = jnp.where(placing, 1.0, 0.0).astype(BF16)
        numbers = jnp.broadcast_to(request.astype(F32), (slots, LANES)).astype(BF16)
        for k in range(groups):
            xsend[h, k, :, depth:] = numbers[k * part:(k + 1) * part]
        for j in range(depth // step):
            moved = jnp.dot(
                place, x_ref[:, j * step:(j + 1) * step], preferred_element_type=F32
            ).astype(BF16)
            for k in range(groups):
                xsend[h, k, :, j * step:(j + 1) * step] = moved[k * part:(k + 1) * part]
        if h == 0:
            pl.semaphore_wait(barrier, chips + groups - 1)
        for k in range(1, groups):
            row_copy(h, k).start()
        xrecv[h, g] = xsend[h, g]
        if h == 0:
            down_copy.start()

    tile = min(256, piece)
    tiles = piece // tile

    def pair_copy(chip, q):
        k = chip * PIECES + q
        return pltpu.make_async_remote_copy(
            src_ref=psend.at[k], dst_ref=precv.at[k], send_sem=ps_sem.at[k],
            recv_sem=pr_sem.at[k], device_id=(g, partner), device_id_type=MESH,
        )

    strip = 16

    def hop(chip, q, to, send, recv, s_sem, r_sem):
        k = chip * PIECES + q
        return pltpu.make_async_remote_copy(
            src_ref=send.at[k], dst_ref=recv.at[k], send_sem=s_sem.at[k],
            recv_sem=r_sem.at[k], device_id=(g, to * 2 + c), device_id_type=MESH,
        )

    right = functools.partial(hop, send=rsend, recv=rrecv, s_sem=rs_sem, r_sem=rr_sem)
    left = functools.partial(hop, send=lsend, recv=lrecv, s_sem=ls_sem, r_sem=lr_sem)

    def pass_on(chip, q, first, to, make, send, recv):
        k = chip * PIECES + q

        @pl.when(first)
        def _():
            @pl.loop(0, rows // strip)
            def _(n):
                at = pl.ds(pl.multiple_of(n * strip, strip), strip)
                send[k, at] = (own[k, at] + precv[k, at].astype(F32)).astype(BF16)

        @pl.when(jnp.logical_not(first))
        def _():
            make(chip, q, to).wait_recv()

            @pl.loop(0, rows // strip)
            def _(n):
                at = pl.ds(pl.multiple_of(n * strip, strip), strip)
                send[k, at] = (
                    own[k, at] + precv[k, at].astype(F32) + recv[k, at].astype(F32)
                ).astype(BF16)

        make(chip, q, to).start()

    def chain(turn, q):
        @pl.when(z <= turn)
        def _():
            pass_on(chips - 1 - turn + z, q, z == 0, z + 1, right, rsend, rrecv)

        @pl.when(chips - 1 - z <= turn)
        def _():
            pass_on(turn - chips + 1 + z, q, z == chips - 1, z - 1, left, lsend, lrecv)

    def start_weights(n):
        if n + AHEAD < members:
            weight_copy(n + AHEAD).start()

    def project(i):
        chip = block_chip(i)
        weight_copy(2 * i).wait()
        start_weights(2 * i)
        for q in range(PIECES):
            for n in range(tiles):
                psend[chip * PIECES + q, :, n * tile:(n + 1) * tile] = jnp.dot(
                    x_ref[...],
                    wbuf[2 * i, :, q * piece + n * tile:q * piece + (n + 1) * tile],
                    preferred_element_type=F32,
                ).astype(BF16)
            pair_copy(chip, q).start()
        weight_copy(2 * i + 1).wait()
        start_weights(2 * i + 1)
        for q in range(PIECES):
            for n in range(tiles):
                own[chip * PIECES + q, :, n * tile:(n + 1) * tile] = jnp.dot(
                    x_ref[...],
                    wbuf[2 * i + 1, :, q * piece + n * tile:q * piece + (n + 1) * tile],
                    preferred_element_type=F32,
                )
            if i == 0:
                pair_copy(chip, q).wait_recv()
                if chips > 1:
                    chain(0, q)

    def paired(i):
        for q in range(PIECES):
            pair_copy(block_chip(i), q).wait_recv()

    lane_group = lax.broadcasted_iota(jnp.int32, (slots, LANES), 1) // rank
    lane_number = (lane_group + 1).astype(F32)
    per_tile = LANES // rank
    tile_count = owned * rank // LANES
    pair = 2 if tile_count % 2 == 0 else 1
    pack_rows = slots // per_tile
    pack_group = lax.broadcasted_iota(jnp.int32, (pack_rows, LANES), 1) // rank

    def spread_lanes(v):
        shift = rank
        while shift < LANES:
            v = v + pltpu.roll(v, shift, 1)
            shift *= 2
        return v

    def term_pair(h):
        return pltpu.make_async_remote_copy(
            src_ref=packed.at[h], dst_ref=arp.at[h], send_sem=as_sem.at[h],
            recv_sem=ar_sem.at[h], device_id=(g, partner), device_id_type=MESH,
        )

    def term_copy(h, k):
        to = lax.rem(z + k, chips)
        return pltpu.make_async_remote_copy(
            src_ref=arz.at[h, z], dst_ref=arz.at[h, z], send_sem=zs_sem.at[h * chips + k],
            recv_sem=zr_sem.at[h * chips + z], device_id=(g, to * 2 + c), device_id_type=MESH,
        )

    def term_wait(h, k):
        source = lax.rem(z + k, chips)
        pltpu.make_async_remote_copy(
            src_ref=arz.at[h, source], dst_ref=arz.at[h, source],
            send_sem=zs_sem.at[h * chips + k], recv_sem=zr_sem.at[h * chips + source],
            device_id=(g, source * 2 + c), device_id_type=MESH,
        ).wait_recv()

    def wanted_of(h):
        return xrecv[h, :, :, depth:].reshape(slots, LANES).astype(F32)

    def shrink_rows(h):
        for k in range(1, groups):
            row_wait(h, k)
        if h == 0:
            down_copy.wait()
            up_copy.start()
            res_copy.start()
        wanted = wanted_of(h)
        flat = xrecv[h, :, :, :depth].reshape(slots, depth)
        terms[...] = jnp.zeros_like(terms)

        @pl.loop(0, tile_count // pair)
        def _(m):
            at = pl.ds(pl.multiple_of(m * pair * LANES, LANES), pair * LANES)
            every = lax.dot_general(
                flat, dbuf[at, :], (((1,), (1,)), ((), ())), preferred_element_type=F32
            )
            for p in range(pair):
                first_number = ((m * pair + p) * per_tile).astype(F32)
                terms[...] += jnp.where(
                    wanted == lane_number + first_number, every[:, p * LANES:(p + 1) * LANES], 0.0
                )

        chosen_terms = spread_lanes(terms[...])
        mine = jnp.zeros((pack_rows, LANES), F32)
        for p in range(per_tile):
            mine = jnp.where(
                pack_group == p, chosen_terms[p * pack_rows:(p + 1) * pack_rows], mine
            )
        packed[h] = mine
        term_pair(h).start()

    def sum_send(h):
        term_pair(h).wait_recv()
        arz[h, z] = packed[h] + arp[h]
        for k in range(1, chips):
            term_copy(h, k).start()

    def back_copy(h, k):
        to = lax.rem(g + k, groups)
        return pltpu.make_async_remote_copy(
            src_ref=esend.at[h, to], dst_ref=eback.at[h, g],
            send_sem=es_sem.at[h * groups + k], recv_sem=er_sem.at[h * groups + g],
            device_id=(to, t), device_id_type=MESH,
        )

    def back_wait(h, k):
        source = lax.rem(g + k, groups)
        pltpu.make_async_remote_copy(
            src_ref=esend.at[h, source], dst_ref=eback.at[h, source],
            send_sem=es_sem.at[h * groups + k], recv_sem=er_sem.at[h * groups + source],
            device_id=(source, t), device_id_type=MESH,
        ).wait_recv()

    wide = min(256, width)

    def expand_rows(h):
        for k in range(1, chips):
            term_wait(h, k)
        total = arz[h, 0]
        for k in range(1, chips):
            total = total + arz[h, k]
        total = total.astype(BF16).astype(F32)
        if h == 0:
            up_copy.wait()
        wanted = wanted_of(h)
        shrink = jnp.concatenate(
            [spread_lanes(jnp.where(pack_group == p, total, 0.0)) for p in range(per_tile)],
            axis=0,
        )
        spread = jnp.concatenate(
            [
                jnp.where(wanted == lane_number + float(m * per_tile), shrink, 0.0).astype(BF16)
                for m in range(tile_count)
            ],
            axis=1,
        )

        @pl.loop(0, width // wide)
        def _(n):
            cols = pl.ds(pl.multiple_of(n * wide, LANES), wide)
            grown = jnp.dot(spread, ubuf[:, cols], preferred_element_type=F32).astype(BF16)
            for k in range(groups):
                esend[h, k, :, cols] = grown[k * part:(k + 1) * part]

        for k in range(1, groups):
            back_copy(h, k).start()
        eback[h, g] = esend[h, g]

    last = halves - 1
    early = chips // 2
    project(0)
    if chips > 1:
        project(1)
    shrink_rows(0)
    for i in range(2, chips):
        project(i)
        paired(i - 1)
        if i == 2:
            sum_send(0)
        if i - 1 < early and i - 1 < chips - 1:
            chain(i - 1, 0)
        if i == 2 and halves > 1:
            shrink_rows(1)
        if i - 1 < early and i - 1 < chips - 1:
            for q in range(1, PIECES):
                chain(i - 1, q)
    if chips > 1:
        paired(chips - 1)
    if chips < 3:
        sum_send(0)
        if halves > 1:
            shrink_rows(1)
    if halves > 1:
        sum_send(1)
    expand_rows(0)
    for turn in range(early, chips - 1):
        chain(turn, 0)
    if halves > 1:
        expand_rows(1)
    for turn in range(early, chips - 1):
        for q in range(1, PIECES):
            chain(turn, q)

    res_copy.wait()

    def branch_of(h, q, n):
        slot_col = slot_of(rank_col, own_col, h)
        unplace = jnp.where(
            lax.broadcasted_iota(jnp.int32, (rows, slots), 1) == slot_col, 1.0, 0.0
        ).astype(BF16)
        first = q * piece + n * tile
        back = eback[h, :, :, first:first + tile].reshape(slots, tile)
        return jnp.dot(unplace, back, preferred_element_type=F32)

    for h in range(halves):
        for k in range(1, groups):
            back_wait(h, k)
        for q in range(PIECES):
            for n in range(tiles):
                cols = slice(n * tile, (n + 1) * tile)
                first = q * piece + n * tile
                value = own[z * PIECES + q, :, cols] + branch_of(h, q, n)
                if h == 0:
                    value = (
                        value + precv[z * PIECES + q, :, cols].astype(F32)
                        + rbuf[:, first:first + tile].astype(F32)
                    )
                own[z * PIECES + q, :, cols] = value

    for q in range(PIECES):
        mine_at = z * PIECES + q

        def finish(use_right, use_left):
            @pl.loop(0, rows // strip)
            def _(n):
                at = pl.ds(pl.multiple_of(n * strip, strip), strip)
                value = own[mine_at, at]
                if use_right:
                    value = value + rrecv[mine_at, at].astype(F32)
                if use_left:
                    value = value + lrecv[mine_at, at].astype(F32)
                out_ref[at, q * piece:(q + 1) * piece] = value.astype(BF16)

        if chips == 1:
            finish(False, False)
        else:
            @pl.when(z == 0)
            def _():
                left(z, q, z).wait_recv()
                finish(False, True)

            @pl.when(z == chips - 1)
            def _():
                right(z, q, z).wait_recv()
                finish(True, False)

            @pl.when((z > 0) & (z < chips - 1))
            def _():
                right(z, q, z).wait_recv()
                left(z, q, z).wait_recv()
                finish(True, True)

    for i in range(chips):
        for q in range(PIECES):
            pair_copy(i, q).wait_send()
    for h in range(halves):
        for k in range(1, groups):
            row_copy(h, k).wait_send()
            back_copy(h, k).wait_send()
        term_pair(h).wait_send()
        for k in range(1, chips):
            term_copy(h, k).wait_send()
    for chip in range(chips):
        for q in range(PIECES):
            @pl.when(z < chip)
            def _():
                right(chip, q, z + 1).wait_send()

            @pl.when(z > chip)
            def _():
                left(chip, q, z - 1).wait_send()


def body(attention_output, residual, output_weight, down_factors, up_factors, adapter_index):
    groups = lax.axis_size("dp")
    members = lax.axis_size("tensor")
    rows, depth = attention_output.shape
    owned, _, rank = down_factors.shape
    width = output_weight.shape[1] // members
    cap = 2 * rows // groups
    chips = members // 2
    halves = 2 if cap % 32 == 0 else 1
    part = cap // halves
    slots = groups * part
    pack = slots * rank // LANES
    piece = width // PIECES
    down = jnp.swapaxes(down_factors, 1, 2).reshape(owned * rank, depth)
    up = up_factors.reshape(owned * rank, width)
    vmem = pl.BlockSpec(memory_space=pltpu.VMEM)
    hbm = pl.BlockSpec(memory_space=pl.ANY)
    dma = pltpu.SemaphoreType.DMA
    hops = chips * PIECES
    return pl.pallas_call(
        functools.partial(kernel, groups, members, rank, owned, halves),
        out_shape=jax.ShapeDtypeStruct((rows, width), BF16),
        in_specs=[vmem, hbm, vmem, hbm, hbm, hbm],
        out_specs=vmem,
        scratch_shapes=[
            pltpu.VMEM((members, depth, width), BF16),
            pltpu.VMEM((owned * rank, depth), BF16),
            pltpu.VMEM((owned * rank, width), BF16),
            pltpu.VMEM((rows, width), BF16),
            pltpu.VMEM((hops, rows, piece), F32),
            pltpu.VMEM((hops, rows, piece), BF16),
            pltpu.VMEM((hops, rows, piece), BF16),
            pltpu.VMEM((hops, rows, piece), BF16),
            pltpu.VMEM((hops, rows, piece), BF16),
            pltpu.VMEM((hops, rows, piece), BF16),
            pltpu.VMEM((hops, rows, piece), BF16),
            pltpu.VMEM((halves, groups, part, depth + LANES), BF16),
            pltpu.VMEM((halves, groups, part, depth + LANES), BF16),
            pltpu.VMEM((slots, LANES), F32),
            pltpu.VMEM((halves, pack, LANES), F32),
            pltpu.VMEM((halves, pack, LANES), F32),
            pltpu.VMEM((halves, chips, pack, LANES), F32),
            pltpu.VMEM((halves, groups, part, width), BF16),
            pltpu.VMEM((halves, groups, part, width), BF16),
            dma((members,)), dma((3,)),
            dma((hops,)), dma((hops,)),
            dma((hops,)), dma((hops,)), dma((hops,)), dma((hops,)),
            dma((halves * groups,)), dma((halves * groups,)),
            dma((halves,)), dma((halves,)),
            dma((halves * chips,)), dma((halves * chips,)),
            dma((halves * groups,)), dma((halves * groups,)),
        ],
        compiler_params=pltpu.CompilerParams(
            collective_id=0, has_side_effects=True, vmem_limit_bytes=60 * 1024 * 1024
        ),
    )(attention_output, residual, adapter_index.reshape(1, rows), output_weight, down, up)


def solution(mesh):
    return jax.shard_map(
        body,
        mesh=mesh,
        in_specs=(
            P("dp", "tensor"),
            P("dp", "tensor"),
            P("tensor", None),
            P("dp", "tensor", None),
            P("dp", None, "tensor"),
            P("dp"),
        ),
        out_specs=P("dp", "tensor"),
        check_vma=False,
    )
```

time: 96.7 us -> 34.1 us (0.35)
  Pallas kernels: 0 us -> 32.2 us
  blocking collectives: 28 us -> 0 us
  matrix products: 20.9 us -> 0 us
  waiting for transfers between devices: 16.5 us -> 0 us
  between operations: 13.5 us -> 0.01 us
  starting transfers between devices: 12.1 us -> 0 us
  other arithmetic: 1.86 us -> 0 us
  local copies, waits for them, and re-layouts: 3.45 us -> 1.67 us
    pallas_call x0 -> x1, Pallas kernels: none -> 32.2 us  [body(): pl.pallas_call(functools.partial(kernel, groups, members, rank, owned, ha...]
    psum x1 -> x0, blocking collectives: 28 us -> none  [body(): shrink = lax.psum(shrink, 'tensor').astype(jnp.bfloat16)]
    dot_general x4 -> x0, matrix products: 20.9 us -> none  [the longest x1 12.4 us: body(): lax.dot_general(output_weight, attention_output, (((0,), (1,)), ((), ()))...]
    all_to_all x3 -> x0, waiting for transfers between devices: 16.5 us -> none  [the longest x1 6.67 us: body(): lax.all_to_all(outgoing, 'dp', split_axis=0, concat_axis=0, tiled=True)]
    all_to_all x3 -> x0, starting transfers between devices: 12.1 us -> none  [the longest x1 5.19 us: body(): lax.all_to_all(request, 'dp', split_axis=0, concat_axis=0, tiled=True)]
    convert_element_type x2 -> x0, local copies, waits for them, and re-layouts: 1.52 us -> none  [the longest x1 0.85 us: body(): return total.astype(jnp.bfloat16)]
    convert_element_type x5 -> x0, other arithmetic: 1.34 us -> none  [the longest x1 1.17 us: body(): return total.astype(jnp.bfloat16)]
    gather x2 -> x0, local copies, waits for them, and re-layouts: 1.03 us -> none  [body(): jnp.take(returned.reshape(slot_count, column_count), row_slot, axis=0)]
  transfers between devices with their start and end apart: 4 -> 0, of which waited for: 3 -> 0; matrix products, arithmetic and copies ran while one was open for 12% -> 0% of each run, Pallas kernels for 0% -> 0%
where the time goes in v2:
time: 34.1 us; the launch traced here: 33.9 us
  Pallas kernels  32.2 us (94%)
  local copies, waits for them, and re-layouts  1.67 us (5%)
    pallas_call x1, Pallas kernels, body(): pl.pallas_call(functools.partial(kernel, groups, members, rank, owned, ha...  32.2 us
    unnamed x1, local copies, waits for them, and re-layouts  1.67 us

profile of v2, /device:TPU:0, one launch (start us, length us, event | category | flops | bytes accessed | tf_op | source)
XLA Modules:
  0.0 33.9 jit_solution(17365075129733881543)
XLA Ops:
  0.0 32.2 %shard_map.64 = bf16[128,1024]{1,0:T(8,128)(2,1)} custom-call(bf16[128,1024]{1,0:T(8,128)(2,1)} %x_ref.1, bf16[128,1024]{1,0:T(8,128)(2,1)} %res_ref.1, s32[1,128]{1,0:T(1,128)} %bitcast.7, bf16[1024,8192]{1,0:T(8,128)(2,1)} %w_ref.1, bf16[1024,1024]{1,0:T(8,128)(2,1)} %bitcast.5, bf16[1024,1024]{1,0:T(8,128)(2,1)} %bitcast.6), custom_call_target="tpu_custom_call" | custom-call | tf_op jit(solution)/shard_map/pallas_call | solution.py:473
  32.2 1.7 %copy.8 = bf16[128,1024]{1,0:T(8,128)(2,1)} copy(bf16[128,1024]{1,0:T(8,128)(2,1)} %shard_map.64) | data formatting | bytes 524288
